TPU v7x, 32 devices: a whole 2x2x4 slice. The times are simulated.
32 devices in a mesh: group: 8 (over z, core), member: 4 (over y, x).
Axes of the slice: x: 2, y: 2, z: 4, core: 2. Of those that a mesh axis runs over, the one named last changes fastest.
Arguments:
- rhs: bfloat16 [8, 4, 768, 128], P('group', 'member'), may hold values from -6 to 6
- leaf_pivot_inverse: bfloat16 [8, 4, 768, 768], P('group', 'member'), may hold values from -1.5 to 1.5, as said below
- leaf_border_block: bfloat16 [8, 4, 512, 768], P('group', 'member'), may hold values from -0.21875 to 0.21875
- leaf_map: int32 [8, 4, 4], P('group'), may hold values from 0 to 47, as said below
- mid_inverse: bfloat16 [8, 2048, 2048], P('group', 'member'), may hold values from -1.5 to 1.5, as said below
- mid_border: bfloat16 [8, 4096, 2048], P('group', None, 'member'), may hold values from -0.125 to 0.125
- root_map: int32 [8, 4, 8], P('group', 'member'), may hold values from 0 to 15, as said below
- root_inverse: bfloat16 [8192, 8192], P('group', 'member'), may hold values from -0.5 to 0.5, as said below
Outputs:
- leaf_solution: bfloat16 [8, 4, 768, 128], P('group', 'member')
- mid_solution: bfloat16 [8, 2048, 128], P('group', 'member')
- root_solution: bfloat16 [4, 2048, 128], P('member', 'group')
Inputs may be any that keep to these rules, and one draw needn't show every extreme that they name: `leaf_map`: for each (g, m) the 4 entries are distinct; a value k below 16 names pivot block k of the mid-level front, a larger one border block k - 16. `root_map`: for each (g, m) the entries are distinct. `leaf_pivot_inverse`: each [768, 768] matrix is lower triangular with a positive diagonal, as the inverse of a Cholesky factor is: every entry above the diagonal is zero. `mid_inverse`: each [2048, 2048] matrix is lower triangular with a positive diagonal, as the inverse of a Cholesky factor is: every entry above the diagonal is zero. `root_inverse`: lower triangular with a positive diagonal, as the inverse of a Cholesky factor is: every entry above the diagonal is zero.
All inputs are finite; a program needn't handle non-finite values.
Results may differ from a plain program's by a relative error of at most 0.028.
Values may be sent and summed in bfloat16 or wider, within the bound.
No kernel may reach another device: no remote copies, remote signals or barrier semaphores. Data moves between devices by JAX's collectives and lax.ppermute only.
A program may use at most 64 MiB of HBM per device.

v0:
```python
import jax
import jax.numpy as jnp
from jax import lax
from jax.sharding import PartitionSpec as P

BLOCK = 128


def assemble(block_ids, targets, source_terms):
    selection_mask = (block_ids[:, None] == targets[None, :]).astype(jnp.bfloat16)
    return jnp.einsum(
        "ng,gcy->ncy", selection_mask, source_terms, preferred_element_type=jnp.float32
    )


def transposed(matrix, values):
    return lax.dot_general(
        matrix, values, (((0,), (0,)), ((), ())), preferred_element_type=jnp.float32
    )


def on_device(
    rhs,
    leaf_pivot_inverse,
    leaf_border_block,
    leaf_map,
    mid_inverse,
    mid_border,
    root_map,
    root_inverse,
):
    members = lax.axis_size("member")
    member = lax.axis_index("member")
    leaf_source = rhs[0, 0]
    leaf_cholesky_factor = leaf_pivot_inverse[0, 0]
    leaf_edge = leaf_border_block[0, 0]
    columns = leaf_source.shape[1]
    leaf_blocks = leaf_edge.shape[0] // BLOCK
    own_pivots = mid_inverse.shape[1]
    pivots = mid_inverse.shape[2]
    border_rows = mid_border.shape[1]
    pivot_blocks = pivots // BLOCK
    front_blocks = pivot_blocks + border_rows // BLOCK
    own_border = border_rows // members
    per_member = own_border // BLOCK
    group_maps = leaf_map[0]
    own_targets = lax.dynamic_index_in_dim(group_maps, member, 0, keepdims=False)
    pivot_ids = jnp.arange(pivot_blocks, dtype=jnp.int32)
    mid_factor = mid_inverse[0]
    mid_edge = mid_border[0]
    leaf_forward_solve = jnp.dot(
        leaf_cholesky_factor, leaf_source, preferred_element_type=jnp.float32
    ).astype(jnp.bfloat16)
    leaf_output = (
        -jnp.dot(leaf_edge, leaf_forward_solve, preferred_element_type=jnp.float32)
    ).astype(jnp.bfloat16)
    gathered = lax.all_gather(
        leaf_output.reshape(1, leaf_blocks, BLOCK, columns), "member", axis=0, tiled=True
    )
    source_terms = gathered.reshape(members * leaf_blocks, BLOCK, columns)
    targets = group_maps.reshape(members * leaf_blocks)
    mid_rhs = (
        assemble(pivot_ids, targets, source_terms).reshape(pivots, columns).astype(jnp.bfloat16)
    )
    border_ids = pivot_blocks + member * per_member + jnp.arange(per_member, dtype=jnp.int32)
    leaf_part = assemble(border_ids, targets, source_terms).reshape(own_border, columns)
    mid_forward = jnp.dot(mid_factor, mid_rhs, preferred_element_type=jnp.float32).astype(
        jnp.bfloat16
    )
    partial_update = -jnp.dot(mid_edge, mid_forward, preferred_element_type=jnp.float32)
    mid_update = (
        lax.psum_scatter(
            partial_update.astype(jnp.bfloat16), "member", scatter_dimension=0, tiled=True
        ).astype(jnp.float32)
        + leaf_part
    )
    share_rows = root_inverse.shape[1]
    root_per = share_rows // BLOCK
    chooser = (root_map[0, 0][:, None] == jnp.arange(root_per, dtype=jnp.int32)[None, :]).astype(
        jnp.float32
    )
    root_term = jnp.einsum(
        "iq,ix->qx",
        chooser,
        mid_update.reshape(per_member, BLOCK * columns),
        precision=lax.Precision.HIGHEST,
    )
    root_rhs = (
        lax.psum(root_term.astype(jnp.bfloat16), "group")
        .astype(jnp.float32)
        .reshape(share_rows, columns)
        .astype(jnp.bfloat16)
    )
    root_part = jnp.dot(root_inverse, root_rhs, preferred_element_type=jnp.float32)
    root_forward = lax.psum(root_part.astype(jnp.bfloat16), "member")
    back_part = transposed(root_inverse, root_forward)
    root_values = lax.psum(back_part.astype(jnp.bfloat16), "group")
    rows_out = share_rows // lax.axis_size("group")
    root_out = lax.dynamic_slice_in_dim(
        root_values, lax.axis_index("group") * rows_out, rows_out, 0
    )[None]
    own_values = jnp.einsum(
        "iq,qx->ix",
        chooser.astype(jnp.bfloat16),
        root_values.reshape(root_per, BLOCK * columns),
        preferred_element_type=jnp.float32,
    )
    own_values = own_values.astype(jnp.bfloat16).reshape(own_border, columns)
    border_values = lax.all_gather(own_values, "member", axis=0, tiled=True)
    mid_back = (mid_forward.astype(jnp.float32) - transposed(mid_edge, border_values)).astype(
        jnp.bfloat16
    )
    mid_part = transposed(mid_factor, mid_back)
    mid_values = lax.psum(mid_part.astype(jnp.bfloat16), "member")
    mid_out = lax.dynamic_slice_in_dim(mid_values, member * own_pivots, own_pivots, 0)[None]
    front_values = jnp.concatenate([mid_values, border_values], axis=0).reshape(
        front_blocks, BLOCK, columns
    )
    all_blocks = jnp.arange(front_blocks, dtype=jnp.int32)
    selected_items = (
        assemble(own_targets, all_blocks, front_values)
        .astype(jnp.bfloat16)
        .reshape(leaf_edge.shape[0], columns)
    )
    leaf_backward_solve = (
        leaf_forward_solve.astype(jnp.float32) - transposed(leaf_edge, selected_items)
    ).astype(jnp.bfloat16)
    leaf_value_rows = transposed(leaf_cholesky_factor, leaf_backward_solve).astype(jnp.bfloat16)
    return (leaf_value_rows[None, None], mid_out, root_out)


def solution(mesh):
    in_specs = (
        P("group", "member", None, None),
        P("group", "member", None, None),
        P("group", "member", None, None),
        P("group", None, None),
        P("group", "member", None),
        P("group", None, "member"),
        P("group", "member", None),
        P("group", "member"),
    )
    out_specs = (
        P("group", "member", None, None),
        P("group", "member", None),
        P("member", "group", None),
    )
    return jax.shard_map(
        on_device, mesh=mesh, in_specs=in_specs, out_specs=out_specs, check_vma=False
    )
```

profile of v0, /device:TPU:0, one launch (start us, length us, event | category | flops | bytes accessed | tf_op | source)
XLA Modules:
  0.0 320.4 jit_solution(14530798952716888823)
XLA Ops:
  7.2 0.0 copy-start
  7.2 0.0 reduce-scatter.2.cloned.1.call-start
  7.2 0.9 eq.63
  8.1 1.8 fusion.17
  9.9 1.5 fusion.41
  11.4 0.1 copy.42
  11.5 11.5 %all_gather.6 = bf16[4,4,128,128]{3,2,1,0:T(8,128)(2,1)S(1)} all-gather(bf16[1,4,128,128]{3,2,1,0:T(8,128)(2,1)S(1)} %bitcast.105), channel_id=1, replica_groups=mesh['group'=8,'member'=4] {'member'}, dimensions={0}, use_global_device_ids=true | all-gather | bytes 655360 | tf_op jit(solution)/shard_map/all_gather | solution.py:57
  23.1 0.4 copy.27
  23.5 0.0 copy-start.1
  23.5 0.3 convolution_convert_fusion.4
  23.8 0.1 copy.28
  23.9 0.0 copy-done
  23.9 0.8 fusion.32
  24.8 0.9 copy-done.1
  25.7 2.4 fusion.1
  28.1 0.0 reduce-scatter.2.cloned.1.call-update
  28.1 0.0 all-reduce.5.cloned.1.call-start
  28.2 0.7 copy.39
  29.0 0.0 copy-start.3
  29.0 0.3 fusion.53
  29.2 27.3 %reduce-scatter.2.cloned.1.call-done = bf16[1024,128]{0,1:T(8,128)(2,1)} async-done(((bf16[4096,128]{0,1:T(8,128)(2,1)}), bf16[1024,128]{0,1:T(8,128)(2,1)}) %reduce-scatter.2.cloned.1.call-update) | async-done | bytes 262160 | tf_op jit(solution)/shard_map/reduce_scatter | solution.py:72
  56.5 1.1 bitcast_add_fusion
  57.6 0.2 copy.30
  57.8 0.1 reshape.47
  57.9 0.0 copy-done.3
  57.9 0.7 convolution_convert_fusion
  58.6 1.0 convert_element_type.103
  59.7 0.0 all-reduce.5.cloned.1.call-update
  59.7 0.0 all-reduce.7.cloned.1.call-start
  59.7 56.6 %all-reduce.5.cloned.1.call-done = bf16[2048,128]{1,0:T(8,128)(2,1)} async-done(((bf16[2048,128]{1,0:T(8,128)(2,1)}), bf16[2048,128]{1,0:T(8,128)(2,1)}) %all-reduce.5.cloned.1.call-update) | async-done | bytes 524304 | tf_op jit(solution)/shard_map/psum | solution.py:89
  116.3 4.6 %fusion.24 = bf16[1024,128]{0,1:T(8,128)(2,1)} fusion(bf16[2048,128]{1,0:T(8,128)(2,1)} %all-reduce.5.cloned.1.call-done, bf16[1024,2048]{1,0:T(8,128)(2,1)} %param.15), kind=kOutput, calls=%fused_computation.29 | convolution fusion | flops 537001984 | bytes 4980736 | tf_op jit(solution)/shard_map/dot_general | solution.py:94
  120.9 0.0 all-reduce.7.cloned.1.call-update
  120.9 0.0 all-reduce.9.cloned.1.call-start
  121.0 42.2 %all-reduce.7.cloned.1.call-done = bf16[1024,128]{0,1:T(8,128)(2,1)} async-done(((bf16[1024,128]{0,1:T(8,128)(2,1)}), bf16[1024,128]{0,1:T(8,128)(2,1)}) %all-reduce.7.cloned.1.call-update) | async-done | bytes 262160 | tf_op jit(solution)/shard_map/psum | solution.py:95
  163.2 3.8 %fusion.5 = bf16[2048,128]{0,1:T(8,128)(2,1)} fusion(bf16[1024,128]{0,1:T(8,128)(2,1)} %all-reduce.7.cloned.1.call-done, bf16[1024,2048]{1,0:T(8,128)(2,1)} %param.15), kind=kOutput, calls=%fused_computation.10 | convolution fusion | flops 537133056 | bytes 4980736 | tf_op jit(solution)/shard_map/dot_general | solution.py:17
  167.0 0.0 all-reduce.9.cloned.1.call-update
  167.0 0.0 all-gather.2.cloned.1.call-start
  167.1 56.6 %all-reduce.9.cloned.1.call-done = bf16[2048,128]{0,1:T(8,128)(2,1)} async-done(((bf16[2048,128]{0,1:T(8,128)(2,1)}), bf16[2048,128]{0,1:T(8,128)(2,1)}) %all-reduce.9.cloned.1.call-update) | async-done | bytes 524304 | tf_op jit(solution)/shard_map/psum | solution.py:97
  223.7 1.3 copy.31
  225.0 0.2 reshape.48
  225.2 0.3 convolution_convert_fusion.1
  225.5 0.8 reshape.49
  226.3 0.0 all-gather.2.cloned.1.call-update
  226.3 0.0 all-reduce.11.cloned.1.call-start
  226.4 25.7 %all-gather.2.cloned.1.call-done = bf16[4096,128]{1,0:T(8,128)(2,1)} async-done(((bf16[1024,128]{1,0:T(8,128)(2,1)}), bf16[4096,128]{1,0:T(8,128)(2,1)}) %all-gather.2.cloned.1.call-update) | async-done | bytes 1048592 | tf_op jit(solution)/shard_map/all_gather | solution.py:109
  252.0 4.5 %fusion.6 = bf16[2048,128]{0,1:T(8,128)(2,1)} fusion(bf16[1,512,2048]{2,1,0:T(8,128)(2,1)S(1)} %copy-done, bf16[4096,128]{1,0:T(8,128)(2,1)} %all-gather.2.cloned.1.call-done, bf16[1,4096,512]{2,1,0:T(8,128)(2,1)} %param.13, bf16[128,512]{1,0:T(8,128)(2,1)S(1)} %fusion.32), kind=kOutput, calls=%fused_computation.11 | convolution fusion | flops 805765120 | bytes 7995392 | tf_op jit(solution)/shard_map/dot_general | solution.py:17
  256.5 0.0 all-reduce.11.cloned.1.call-update
  256.5 0.7 fusion.63
  257.2 0.8 constant_dynamic-slice_fusion
  258.1 0.7 copy.37
  258.8 43.3 %all-reduce.11.cloned.1.call-done = bf16[2048,128]{0,1:T(8,128)(2,1)} async-done(((bf16[2048,128]{0,1:T(8,128)(2,1)}), bf16[2048,128]{0,1:T(8,128)(2,1)}) %all-reduce.11.cloned.1.call-update) | async-done | bytes 524304 | tf_op jit(solution)/shard_map/psum | solution.py:114
  302.1 2.0 copy.32
  304.1 0.0 copy-start.2
  304.1 1.6 pad_maximum_fusion
  305.7 1.0 fusion.35
  306.6 0.7 copy.34
  307.3 0.0 copy-done.2
  307.3 2.8 fusion.29
  310.1 1.7 copy.38
  311.8 0.9 constant_dynamic-slice_fusion.1
  312.7 0.8 copy.36
  (1 shorter events, 0.0 us)
Async XLA Ops:
  7.2 16.8 %copy-start = (bf16[1,512,2048]{2,1,0:T(8,128)(2,1)S(1)}, bf16[1,512,2048]{2,1,0:T(8,128)(2,1)}, u32[]{:S(2)}) copy-start(bf16[1,512,2048]{2,1,0:T(8,128)(2,1)} %param.12) | copy-start | bytes 6291460
  7.2 49.4 %reduce-scatter.2.cloned.1.call-start = ((), (), s32[]{:S(2)}) async-start(), calls=%async_computation.1 | async-start | bytes 1310720 | tf_op jit(solution)/shard_map/reduce_scatter | solution.py:72
  23.5 2.2 copy-start.1
  28.1 88.2 %all-reduce.5.cloned.1.call-start = ((), (), s32[]{:S(2)}) async-start(), calls=%async_computation.2 | async-start | bytes 1048576 | tf_op jit(solution)/shard_map/psum | solution.py:89
  29.0 29.0 %copy-start.3 = (s32[1,1,8]{2,1,0:T(1,128)S(1)}, s32[1,1,8]{2,1,0:T(1,128)}, u32[]{:S(2)}) copy-start(s32[1,1,8]{2,1,0:T(1,128)} %param.14) | copy-start | bytes 100
  59.7 103.5 %all-reduce.7.cloned.1.call-start = ((), (), s32[]{:S(2)}) async-start(), calls=%async_computation.3 | async-start | bytes 524288 | tf_op jit(solution)/shard_map/psum | solution.py:95
  120.9 102.7 %all-reduce.9.cloned.1.call-start = ((), (), s32[]{:S(2)}) async-start(), calls=%async_computation.4 | async-start | bytes 1048576 | tf_op jit(solution)/shard_map/psum | solution.py:97
  167.0 85.0 %all-gather.2.cloned.1.call-start = ((), (), s32[]{:S(2)}) async-start(), calls=%async_computation.5 | async-start | bytes 1310720 | tf_op jit(solution)/shard_map/all_gather | solution.py:109
  226.3 75.7 %all-reduce.11.cloned.1.call-start = ((), (), s32[]{:S(2)}) async-start(), calls=%async_computation.6 | async-start | bytes 1048576 | tf_op jit(solution)/shard_map/psum | solution.py:114
  304.1 3.2 copy-start.2
Sparse Core Ops, SparseCore 0:
  28.3 28.2 reduce-scatter.1
  59.8 56.4 all-reduce.4
  121.0 42.0 all-reduce.6
  167.1 56.5 all-reduce.8
  226.5 25.5 all-gather.1
  256.6 45.3 all-reduce.10
where the time goes:
time: 321 us; the launch traced here: 320 us
  waiting for transfers between devices  252 us (79%)
  matrix products  24.6 us (8%)
  local copies, waits for them, and re-layouts  15.3 us (5%)
  between operations  14.3 us (4%)
  blocking collectives  11.5 us (4%)
    psum x1, waiting for transfers between devices, on_device(): root_values = lax.psum(back_part.astype(jnp.bfloat16), 'group')  56.6 us
    psum x1, waiting for transfers between devices, on_device(): lax.psum(root_term.astype(jnp.bfloat16), 'group').astype(jnp.float32)  56.6 us
    psum x1, waiting for transfers between devices, on_device(): mid_values = lax.psum(mid_part.astype(jnp.bfloat16), 'member')  43.3 us
    psum x1, waiting for transfers between devices, on_device(): root_forward = lax.psum(root_part.astype(jnp.bfloat16), 'member')  42.2 us
    reduce_scatter x1, waiting for transfers between devices, on_device(): lax.psum_scatter(partial_update.astype(jnp.bfloat16), 'member', scatter_d...  27.3 us
    all_gather x1, waiting for transfers between devices, on_device(): border_values = lax.all_gather(own_values, 'member', axis=0, tiled=True)  25.7 us
    all_gather x1, blocking collectives, on_device(): lax.all_gather(leaf_output.reshape(1, leaf_blocks, BLOCK, columns), 'memb...  11.5 us
    dot_general x3, matrix products, transposed(): lax.dot_general(matrix, values, (((0,), (0,)), ((), ())), preferred_eleme...  11 us
  transfers between devices with their start and end apart: 6, of which 6 were waited for; matrix products, arithmetic and copies ran while one was open for 1% of the time, Pallas kernels for 0%

commit v1 on v0

--- a/solution.py
+++ b/solution.py
@@ -106,7 +106,14 @@
         preferred_element_type=jnp.float32,
     )
     own_values = own_values.astype(jnp.bfloat16).reshape(own_border, columns)
-    border_values = lax.all_gather(own_values, "member", axis=0, tiled=True)
+    ring = [own_values]
+    for hop in range(3):
+        ring.append(lax.ppermute(ring[-1], "member", [(dev, (dev + 1) % 4) for dev in range(4)]))
+    border_values = jnp.roll(
+        jnp.concatenate(ring[::-1], axis=0),
+        (lax.axis_index("member") + 1) * ring[0].shape[0],
+        axis=0,
+    )
     mid_back = (mid_forward.astype(jnp.float32) - transposed(mid_edge, border_values)).astype(
         jnp.bfloat16
     )

time: 321 us -> 315 us (0.981)
  waiting for transfers between devices: 252 us -> 244 us
  starting transfers between devices: 0.25 us -> 3.74 us
    all_gather x1 -> x0, waiting for transfers between devices: 25.7 us -> none  [on_device(): border_values = lax.all_gather(own_values, 'member', axis=0, tiled=True)]
    ppermute x0 -> x3, waiting for transfers between devices: none -> 19.1 us  [on_device(): lax.ppermute(ring[-1], 'member', [(dev, (dev + 1) % 4) for dev in range(4)])]
    ppermute x0 -> x3, starting transfers between devices: none -> 3.53 us  [on_device(): lax.ppermute(ring[-1], 'member', [(dev, (dev + 1) % 4) for dev in range(4)])]
  transfers between devices with their start and end apart: 6 -> 8, of which waited for: 6 -> 8; matrix products, arithmetic and copies ran while one was open for 1% -> 1% of each run, Pallas kernels for 0% -> 0%
where the time goes in v1:
time: 315 us
  waiting for transfers between devices  244 us (77%)
  matrix products  24.3 us (8%)
  local copies, waits for them, and re-layouts  14.9 us (5%)
  between operations  14 us (4%)
  blocking collectives  11.5 us (4%)
  starting transfers between devices  3.74 us (1%)
    psum x1, waiting for transfers between devices, on_device(): root_values = lax.psum(back_part.astype(jnp.bfloat16), 'group')  56.6 us
    psum x1, waiting for transfers between devices, on_device(): lax.psum(root_term.astype(jnp.bfloat16), 'group').astype(jnp.float32)  56.6 us
    psum x1, waiting for transfers between devices, on_device(): root_forward = lax.psum(root_part.astype(jnp.bfloat16), 'member')  42.2 us
    psum x1, waiting for transfers between devices, on_device(): mid_values = lax.psum(mid_part.astype(jnp.bfloat16), 'member')  42.1 us
    reduce_scatter x1, waiting for transfers between devices, on_device(): lax.psum_scatter(partial_update.astype(jnp.bfloat16), 'member', scatter_d...  27.3 us
    ppermute x3, waiting for transfers between devices, on_device(): lax.ppermute(ring[-1], 'member', [(dev, (dev + 1) % 4) for dev in range(4)])  19.1 us
    all_gather x1, blocking collectives, on_device(): lax.all_gather(leaf_output.reshape(1, leaf_blocks, BLOCK, columns), 'memb...  11.5 us
    dot_general x3, matrix products, transposed(): lax.dot_general(matrix, values, (((0,), (0,)), ((), ())), preferred_eleme...  10.7 us
  transfers between devices with their start and end apart: 8, of which 8 were waited for; matrix products, arithmetic and copies ran while one was open for 1% of the time, Pallas kernels for 0%

profile of v1, /device:TPU:0, one launch (start us, length us, event | category | flops | bytes accessed | tf_op | source)
XLA Modules:
  0.0 314.8 jit_solution(14553276124780337236)
XLA Ops:
  7.2 0.0 copy-start
  7.2 0.0 reduce-scatter.2.cloned.1.call-start
  7.2 0.9 eq.66
  8.1 1.8 fusion.17
  9.9 1.5 fusion.41
  11.4 0.1 copy.42
  11.5 11.5 %all_gather.3 = bf16[4,4,128,128]{3,2,1,0:T(8,128)(2,1)S(1)} all-gather(bf16[1,4,128,128]{3,2,1,0:T(8,128)(2,1)S(1)} %bitcast.105), channel_id=1, replica_groups=mesh['group'=8,'member'=4] {'member'}, dimensions={0}, use_global_device_ids=true | all-gather | bytes 655360 | tf_op jit(solution)/shard_map/all_gather | solution.py:57
  23.1 0.4 copy.27
  23.5 0.0 copy-start.1
  23.5 0.3 convolution_convert_fusion.4
  23.8 0.1 copy.28
  23.9 0.0 copy-done
  23.9 0.8 fusion.32
  24.8 0.9 copy-done.1
  25.7 2.4 fusion.1
  28.1 0.0 reduce-scatter.2.cloned.1.call-update
  28.1 0.0 all-reduce.5.cloned.1.call-start
  28.2 0.7 copy.39
  29.0 0.0 copy-start.3
  29.0 0.3 fusion.53
  29.2 27.3 %reduce-scatter.2.cloned.1.call-done = bf16[1024,128]{0,1:T(8,128)(2,1)} async-done(((bf16[4096,128]{0,1:T(8,128)(2,1)}), bf16[1024,128]{0,1:T(8,128)(2,1)}) %reduce-scatter.2.cloned.1.call-update) | async-done | bytes 262160 | tf_op jit(solution)/shard_map/reduce_scatter | solution.py:72
  56.5 1.1 bitcast_add_fusion
  57.6 0.2 copy.30
  57.8 0.1 reshape.47
  57.9 0.7 convolution_convert_fusion
  58.6 1.0 convert_element_type.103
  59.7 0.0 all-reduce.5.cloned.1.call-update
  59.7 0.0 all-reduce.7.cloned.1.call-start
  59.7 56.6 %all-reduce.5.cloned.1.call-done = bf16[2048,128]{1,0:T(8,128)(2,1)} async-done(((bf16[2048,128]{1,0:T(8,128)(2,1)}), bf16[2048,128]{1,0:T(8,128)(2,1)}) %all-reduce.5.cloned.1.call-update) | async-done | bytes 524304 | tf_op jit(solution)/shard_map/psum | solution.py:89
  116.3 4.6 %fusion.24 = bf16[1024,128]{0,1:T(8,128)(2,1)} fusion(bf16[2048,128]{1,0:T(8,128)(2,1)} %all-reduce.5.cloned.1.call-done, bf16[1024,2048]{1,0:T(8,128)(2,1)} %param.15), kind=kOutput, calls=%fused_computation.29 | convolution fusion | flops 537001984 | bytes 4980736 | tf_op jit(solution)/shard_map/dot_general | solution.py:94
  120.9 0.0 all-reduce.7.cloned.1.call-update
  120.9 0.0 all-reduce.9.cloned.1.call-start
  121.0 42.2 %all-reduce.7.cloned.1.call-done = bf16[1024,128]{0,1:T(8,128)(2,1)} async-done(((bf16[1024,128]{0,1:T(8,128)(2,1)}), bf16[1024,128]{0,1:T(8,128)(2,1)}) %all-reduce.7.cloned.1.call-update) | async-done | bytes 262160 | tf_op jit(solution)/shard_map/psum | solution.py:95
  163.2 3.8 %fusion.5 = bf16[2048,128]{0,1:T(8,128)(2,1)} fusion(bf16[1024,128]{0,1:T(8,128)(2,1)} %all-reduce.7.cloned.1.call-done, bf16[1024,2048]{1,0:T(8,128)(2,1)} %param.15), kind=kOutput, calls=%fused_computation.10 | convolution fusion | flops 537133056 | bytes 4980736 | tf_op jit(solution)/shard_map/dot_general | solution.py:17
  167.0 0.0 all-reduce.9.cloned.1.call-update
  167.0 0.0 all-reduce.11.cloned.1.call-start
  167.0 56.6 %all-reduce.9.cloned.1.call-done = bf16[2048,128]{0,1:T(8,128)(2,1)} async-done(((bf16[2048,128]{0,1:T(8,128)(2,1)}), bf16[2048,128]{0,1:T(8,128)(2,1)}) %all-reduce.9.cloned.1.call-update) | async-done | bytes 524304 | tf_op jit(solution)/shard_map/psum | solution.py:97
  223.7 1.3 copy.31
  225.0 0.2 reshape.48
  225.2 0.3 convolution_convert_fusion.1
  225.5 0.1 reshape.49
  225.6 1.5 collective-permute-start
  227.1 5.8 %collective-permute-done = bf16[1024,128]{1,0:T(8,128)(2,1)S(1)} collective-permute-done((bf16[1024,128]{1,0:T(8,128)(2,1)S(1)}, bf16[1024,128]{1,0:T(8,128)(2,1)S(1)}, u32[]{:S(2)}, u32[]{:S(2)}) %collective-permute-start) | collective-permute-done | bytes 262176 | tf_op jit(solution)/shard_map/ppermute | solution.py:111
  232.9 1.1 collective-permute-start.1
  234.0 7.0 %collective-permute-done.1 = bf16[1024,128]{1,0:T(8,128)(2,1)S(1)} collective-permute-done((bf16[1024,128]{1,0:T(8,128)(2,1)S(1)}, bf16[1024,128]{1,0:T(8,128)(2,1)S(1)}, u32[]{:S(2)}, u32[]{:S(2)}) %collective-permute-start.1) | collective-permute-done | bytes 262176 | tf_op jit(solution)/shard_map/ppermute | solution.py:111
  241.0 0.9 collective-permute-start.2
  241.9 6.3 %collective-permute-done.2 = bf16[1024,128]{1,0:T(8,128)(2,1)S(1)} collective-permute-done((bf16[1024,128]{1,0:T(8,128)(2,1)S(1)}, bf16[1024,128]{1,0:T(8,128)(2,1)S(1)}, u32[]{:S(2)}, u32[]{:S(2)}) %collective-permute-start.2) | collective-permute-done | bytes 262176 | tf_op jit(solution)/shard_map/ppermute | solution.py:111
  248.6 0.1 constant_dynamic-slice_fusion.2
  248.7 4.2 %fusion.6 = bf16[2048,128]{0,1:T(8,128)(2,1)} fusion(bf16[1,512,2048]{2,1,0:T(8,128)(2,1)S(1)} %copy-done, bf16[4096,128]{1,0:T(8,128)(2,1)S(1)} %constant_dynamic-slice_fusion.2, bf16[1,4096,512]{2,1,0:T(8,128)(2,1)} %param.13, bf16[128,512]{1,0:T(8,128)(2,1)S(1)} %fusion.32), kind=kOutput, calls=%fused_computation.11 | convolution fusion | flops 805765120 | bytes 7995392 | tf_op jit(solution)/shard_map/dot_general | solution.py:17
  252.8 0.0 all-reduce.11.cloned.1.call-update
  252.8 0.7 fusion.63
  253.5 0.8 constant_dynamic-slice_fusion
  254.4 0.7 copy.37
  255.1 42.1 %all-reduce.11.cloned.1.call-done = bf16[2048,128]{0,1:T(8,128)(2,1)} async-done(((bf16[2048,128]{0,1:T(8,128)(2,1)}), bf16[2048,128]{0,1:T(8,128)(2,1)}) %all-reduce.11.cloned.1.call-update) | async-done | bytes 524304 | tf_op jit(solution)/shard_map/psum | solution.py:121
  297.2 2.0 copy.32
  299.3 1.1 pad_maximum_fusion
  300.4 0.0 copy-start.2
  300.4 1.0 fusion.35
  301.4 0.7 copy.34
  302.1 0.0 copy-done.2
  302.1 2.8 fusion.29
  304.8 1.7 copy.38
  306.6 0.9 constant_dynamic-slice_fusion.1
  307.5 0.8 copy.36
  (10 shorter events, 0.3 us)
Async XLA Ops:
  7.2 16.8 %copy-start = (bf16[1,512,2048]{2,1,0:T(8,128)(2,1)S(1)}, bf16[1,512,2048]{2,1,0:T(8,128)(2,1)}, u32[]{:S(2)}) copy-start(bf16[1,512,2048]{2,1,0:T(8,128)(2,1)} %param.12) | copy-start | bytes 6291460
  7.2 49.4 %reduce-scatter.2.cloned.1.call-start = ((), (), s32[]{:S(2)}) async-start(), calls=%async_computation.1 | async-start | bytes 1310720 | tf_op jit(solution)/shard_map/reduce_scatter | solution.py:72
  23.5 2.2 copy-start.1
  28.1 88.2 %all-reduce.5.cloned.1.call-start = ((), (), s32[]{:S(2)}) async-start(), calls=%async_computation.2 | async-start | bytes 1048576 | tf_op jit(solution)/shard_map/psum | solution.py:89
  29.0 29.0 %copy-start.3 = (s32[1,1,8]{2,1,0:T(1,128)S(1)}, s32[1,1,8]{2,1,0:T(1,128)}, u32[]{:S(2)}) copy-start(s32[1,1,8]{2,1,0:T(1,128)} %param.14) | copy-start | bytes 100
  59.7 103.5 %all-reduce.7.cloned.1.call-start = ((), (), s32[]{:S(2)}) async-start(), calls=%async_computation.3 | async-start | bytes 524288 | tf_op jit(solution)/shard_map/psum | solution.py:95
  120.9 102.7 %all-reduce.9.cloned.1.call-start = ((), (), s32[]{:S(2)}) async-start(), calls=%async_computation.4 | async-start | bytes 1048576 | tf_op jit(solution)/shard_map/psum | solution.py:97
  167.0 130.2 %all-reduce.11.cloned.1.call-start = ((), (), s32[]{:S(2)}) async-start(), calls=%async_computation.5 | async-start | bytes 1048576 | tf_op jit(solution)/shard_map/psum | solution.py:121
  225.6 7.3 %collective-permute-start = (bf16[1024,128]{1,0:T(8,128)(2,1)S(1)}, bf16[1024,128]{1,0:T(8,128)(2,1)S(1)}, u32[]{:S(2)}, u32[]{:S(2)}) collective-permute-start(bf16[1024,128]{1,0:T(8,128)(2,1)S(1)} %reshape.49), channel_id=1, source_target_pairs={{0,1},{1,2},{2,3},{3,0},{4,5},{5,6},{6,7},{7,4},{8,9},{9,10},{10,1... | collective-permute-start | bytes 786440 | tf_op jit(solution)/shard_map/ppermute | solution.py:111
  232.9 8.0 %collective-permute-start.1 = (bf16[1024,128]{1,0:T(8,128)(2,1)S(1)}, bf16[1024,128]{1,0:T(8,128)(2,1)S(1)}, u32[]{:S(2)}, u32[]{:S(2)}) collective-permute-start(bf16[1024,128]{1,0:T(8,128)(2,1)S(1)} %collective-permute-done), channel_id=1, source_target_pairs={{0,1},{1,2},{2,3},{3,0},{4,5},{5,6},{6,7},{7,4},{8,9},{9,10},{10,1... | collective-permute-start | bytes 786440 | tf_op jit(solution)/shard_map/ppermute | solution.py:111
  241.0 7.3 %collective-permute-start.2 = (bf16[1024,128]{1,0:T(8,128)(2,1)S(1)}, bf16[1024,128]{1,0:T(8,128)(2,1)S(1)}, u32[]{:S(2)}, u32[]{:S(2)}) collective-permute-start(bf16[1024,128]{1,0:T(8,128)(2,1)S(1)} %collective-permute-done.1), channel_id=1, source_target_pairs={{0,1},{1,2},{2,3},{3,0},{4,5},{5,6},{6,7},{7,4},{8,9},{9,10},{10,1... | collective-permute-start | bytes 786440 | tf_op jit(solution)/shard_map/ppermute | solution.py:111
  300.4 1.6 copy-start.2
Sparse Core Ops, SparseCore 0:
  28.3 28.2 reduce-scatter.1
  59.8 56.4 all-reduce.4
  121.0 42.0 all-reduce.6
  167.1 56.5 all-reduce.8
  253.0 44.2 all-reduce.10
